TPU v7x, 128 devices: a whole 4x4x4 slice. The times are simulated.
128 devices in a mesh: row: 8 (over x, core), col: 16 (over z, y).
Axes of the slice: x: 4, y: 4, z: 4, core: 2. Of those that a mesh axis runs over, the one named last changes fastest.
Arguments:
- fact_keys: int32 [32768], P(('row', 'col')), may hold values from 0 to 524287, as said below
- dim_keys: int32 [524288], P(('row', 'col')), may hold values from 0 to 524287, as said below
- dim_payload: bfloat16 [524288, 256], P(('row', 'col')), may hold values from -6 to 6
Outputs:
- joined: bfloat16 [32768, 256], P(('row', 'col'))
Inputs may be any that keep to these rules, and one draw needn't show every extreme that they name: `fact_keys`: each key names a row of dim_keys. Its partition is key // 65536, and within it the block (key % 65536) // 4096. Among the 256 keys of one device at most 64 lie in one partition, and at most 8 in one block of one partition; in every draw one partition, the same on all devices, receives exactly 64 keys from every device, and some block of it exactly 8 keys from every device. `dim_keys`: the 4096 dimension rows of index r of the row axis and index c of the col axis hold the keys r * 65536 + c * 4096 to r * 65536 + (c + 1) * 4096 - 1, each once, in no particular order.
All inputs are finite; a program needn't handle non-finite values.
Results may differ from a plain program's by a relative error of at most 0.001.
Values may be sent and summed in bfloat16 or wider, within the bound.
A program may use at most 64 MiB of HBM per device.

v0:
```python
import math

import jax
import jax.numpy as jnp
from jax import lax
from jax.sharding import PartitionSpec as P


def match_rows(probe, table_keys, table_rows):
    probe_count = probe.shape[0]
    table_count = table_keys.shape[0]
    feature_width = table_rows.shape[1]
    row_step = math.gcd(probe_count, 512)
    col_step = math.gcd(table_count, 2048)
    probe_blocks = probe.reshape(probe_count // row_step, row_step)
    key_blocks = table_keys.reshape(table_count // col_step, col_step)
    value_blocks = table_rows.reshape(table_count // col_step, col_step, feature_width)

    def one_block(probe_block):

        def add_block(running, block_pair):
            key_block, row_block = block_pair
            matches = (probe_block[:, None] == key_block[None, :]).astype(jnp.bfloat16)
            return (running + jnp.dot(matches, row_block, preferred_element_type=jnp.float32), None)

        running, unused = lax.scan(
            add_block, jnp.zeros((row_step, feature_width), jnp.float32), (key_blocks, value_blocks)
        )
        return running

    return lax.map(one_block, probe_blocks).reshape(probe_count, feature_width)


def on_device(fact_keys, dim_keys, dim_payload):
    row_devices = lax.axis_size("row")
    col_devices = lax.axis_size("col")
    fact_count = fact_keys.shape[0]
    most = 2 * fact_count // row_devices
    local_rows = dim_keys.shape[0]
    part_rows = local_rows * col_devices
    feature_width = dim_payload.shape[1]
    bucket = fact_keys // part_rows
    member = (bucket[:, None] == jnp.arange(row_devices, dtype=jnp.int32)[None, :]).astype(
        jnp.int32
    )
    within = jnp.sum(jnp.cumsum(member, 0) * member, 1) - 1
    placed = bucket * most + within
    outgoing = (
        jnp.full((row_devices * most,), -1, jnp.int32)
        .at[placed]
        .set(fact_keys)
        .reshape(row_devices, most)
    )
    incoming = lax.all_to_all(outgoing, "row", split_axis=0, concat_axis=0, tiled=True).reshape(
        row_devices * most
    )
    sub_most = max(2, 2 * (most // col_devices))
    slots = row_devices * sub_most
    valid = incoming >= 0
    owner = jnp.where(valid, incoming % part_rows // local_rows, 0)
    owned = (
        (owner[:, None] == jnp.arange(col_devices, dtype=jnp.int32)[None, :]) & valid[:, None]
    ).astype(jnp.int32)
    slot_rank = jnp.sum(jnp.cumsum(owned, 0) * owned, 1) - 1
    target = jnp.where(valid, owner * slots + slot_rank, col_devices * slots)
    requests = jnp.full((col_devices * slots + 1,), -1, jnp.int32).at[target].set(incoming)
    requests = requests[: col_devices * slots].reshape(col_devices, slots)
    asked = lax.all_to_all(requests, "col", split_axis=0, concat_axis=0, tiled=True)
    item_count = asked.shape[1]
    found = match_rows(asked.reshape(col_devices * item_count), dim_keys, dim_payload).astype(
        jnp.bfloat16
    )
    found = found.reshape(col_devices, item_count, feature_width)
    answered = lax.all_to_all(found, "col", split_axis=0, concat_axis=0, tiled=True)
    flat_rows = answered.reshape(col_devices * slots, feature_width)
    fetched = flat_rows[jnp.where(valid, target, 0)]
    looked_up = jnp.where(valid[:, None], fetched.astype(jnp.float32), 0.0)
    answers = looked_up.astype(jnp.bfloat16).reshape(row_devices, most, feature_width)
    returned = lax.all_to_all(answers, "row", split_axis=0, concat_axis=0, tiled=True).reshape(
        row_devices * most, feature_width
    )
    return returned[placed]


def solution(mesh):
    return jax.shard_map(
        on_device,
        mesh=mesh,
        in_specs=(P(("row", "col")), P(("row", "col")), P(("row", "col"), None)),
        out_specs=P(("row", "col"), None),
        check_vma=False,
    )
```

profile of v0, /device:TPU:1, one launch (start us, length us, event | category | flops | bytes accessed | tf_op | source)
XLA Modules:
  0.0 76.2 jit_solution(14605805617582894295)
XLA Ops:
  0.0 0.7 fusion.31
  0.7 0.7 and_select_fusion.2
  1.4 0.6 reduce-window.14
  2.3 0.7 compare_select_fusion.7
  3.0 1.6 %scatter_custom_fusion = s32[512]{0:T(512)S(1)} fusion(s32[256]{0:T(256)S(1)} %compare_select_fusion.7, s32[256]{0:T(256)} %param.7, s32[]{:T(128)} %constant.79.clone.1), kind=kCustom, calls=%fused_computation.81 | custom fusion | bytes 2560 | tf_op jit(solution)/shard_map/scatter | solution.py:51
  4.7 10.2 %all_to_all.28 = s32[8,1,64]{2,1,0:T(1,128)S(1)} all-to-all(s32[8,1,64]{2,1,0:T(1,128)S(1)} %all_to_all.18), channel_id=1, replica_groups=mesh['row'=8,'col'=16] {'row'}, dimensions={0} | all-to-all | bytes 4096 | tf_op jit(solution)/shard_map/all_to_all | solution.py:54
  15.1 1.2 %reduce-window.16 = s32[16,4,128]{2,0,1:T(8,128)S(1)} reduce-window(s32[16,4,128]{2,0,1:T(8,128)S(1)} %fusion.15, s32[]{:T(128)} %constant.81.clone.1), window={size=1x1x128 pad=0_0x0_0x127_0}, to_apply=%region_4.5 | reduce-window | flops 1040384 | bytes 65540 | tf_op jit(solution)/shard_map/reduce-window.2
  16.2 0.2 slice_reduce_fusion
  16.6 0.5 broadcast.410
  17.1 0.6 reduce.14
  17.8 2.5 %scatter_custom_fusion.1 = s32[1025]{0:T(1024)S(1)} fusion(s32[512]{0:T(512)S(1)} %bitcast.61, s32[512]{0:T(512)S(1)} %reshape.307, s32[]{:T(128)} %constant.79.clone.1), kind=kCustom, calls=%fused_computation.44 | custom fusion | bytes 4104 | tf_op jit(solution)/shard_map/scatter | solution.py:66
  20.3 0.7 all_to_all.20
  20.9 7.8 %all-to-all-start.1 = ((s32[16,1,64]{2,1,0:T(1,128)}), s32[16,1,64]{2,1,0:T(1,128)S(1)}, u32[]{:S(2)}, u32[]{:S(2)}) async-start(s32[16,1,64]{2,1,0:T(1,128)} %all_to_all.20), calls=%async_computation.1 | async-start | bytes 16384 | tf_op jit(solution)/shard_map/all_to_all | solution.py:68
  28.7 0.7 reshape.274
  29.5 5.6 %all-to-all-done.1 = s32[16,1,64]{2,1,0:T(1,128)S(1)} async-done(((s32[16,1,64]{2,1,0:T(1,128)}), s32[16,1,64]{2,1,0:T(1,128)S(1)}, u32[]{:S(2)}, u32[]{:S(2)}) %all-to-all-start.1) | async-done | bytes 4128 | tf_op jit(solution)/shard_map/all_to_all | solution.py:68
  35.1 0.6 reduce.15
  35.8 9.9 %while.22 = (s32[]{:T(128)}, bf16[2,512,256]{2,1,0:T(8,128)(2,1)}, s32[2,512]{1,0:T(2,128)S(1)}, s32[2,2048]{1,0:T(2,128)S(1)}, bf16[2,2048,256]{2,1,0:T(8,128)(...) while((s32[]{:T(128)}, bf16[2,512,256]{2,1,0:T(8,128)(2,1)}, s32[2,512]{1,0:T(2,128)S(1)}, ...), condition=%wide.region_11.12_spmd, body=%wide.region_8.11_spmd.sunk | while | flops 538181632 | bytes 3177724 | solution.py:31
  35.8 4.2 %while.23 = (s32[]{:T(128)}, f32[512,256]{1,0:T(8,128)S(1)}, s32[512]{0:T(512)S(1)}, s32[2,2048]{1,0:T(2,128)S(1)}, bf16[2,2048,256]{2,1,0:T(8,128)(2,1)}, /*index=5*/s32[]{:T(128)}, s32[]{:T(128)}) while((s32[]{:T(128)}, f32[512,256]{1,0:T(8,128)S(1)}, s32[512]{0:T(512)S(1)}, s32[2,2048]{1,0:T(2,128)S(1)}, ...), condition=%wide.region_10.10_spmd.clone, body=%wide.region_9.9_spmd.clone.sunk | while | flops 538181632 | bytes 2124379 | solution.py:26
  35.8 2.1 %fusion.37 = f32[512,256]{1,0:T(8,128)S(1)} fusion(s32[2048]{0:T(1024)S(1)} %bitcast.53, s32[512]{0:T(512)S(1)} %get-tuple-element.191, bf16[2,2048,256]{2,1,0:T(8,128)(2,1)} %get-tuple-element.193, s32[]{:T(128)} %get-tuple-element.182, f32[512,256]{1,0:T(8,128)S(1)} %get-tuple-element.183, pred[]{:T(512)S(6)} %compare.38), kind=kOutput, calls=%fused_computation.8.clone.1 | convolution fusion | flops 538181632 | bytes 2107905 | tf_op jit(solution)/shard_map/while/body/eval_jaxpr/while/body/eval_jaxpr/dot_general | solution.py:24
  37.9 2.1 %fusion.37 = f32[512,256]{1,0:T(8,128)S(1)} fusion(s32[2048]{0:T(1024)S(1)} %bitcast.53, s32[512]{0:T(512)S(1)} %get-tuple-element.191, bf16[2,2048,256]{2,1,0:T(8,128)(2,1)} %get-tuple-element.193, s32[]{:T(128)} %get-tuple-element.182, f32[512,256]{1,0:T(8,128)S(1)} %get-tuple-element.183, pred[]{:T(512)S(6)} %compare.38), kind=kOutput, calls=%fused_computation.8.clone.1 | convolution fusion | flops 538181632 | bytes 2107905 | tf_op jit(solution)/shard_map/while/body/eval_jaxpr/while/body/eval_jaxpr/dot_general | solution.py:24
  40.0 0.7 bitcast_dynamic-update-slice_fusion.2
  40.7 4.2 %while.23 = (s32[]{:T(128)}, f32[512,256]{1,0:T(8,128)S(1)}, s32[512]{0:T(512)S(1)}, s32[2,2048]{1,0:T(2,128)S(1)}, bf16[2,2048,256]{2,1,0:T(8,128)(2,1)}, /*index=5*/s32[]{:T(128)}, s32[]{:T(128)}) while((s32[]{:T(128)}, f32[512,256]{1,0:T(8,128)S(1)}, s32[512]{0:T(512)S(1)}, s32[2,2048]{1,0:T(2,128)S(1)}, ...), condition=%wide.region_10.10_spmd.clone, body=%wide.region_9.9_spmd.clone.sunk | while | flops 538181632 | bytes 2124379 | solution.py:26
  40.8 2.1 %fusion.37 = f32[512,256]{1,0:T(8,128)S(1)} fusion(s32[2048]{0:T(1024)S(1)} %bitcast.53, s32[512]{0:T(512)S(1)} %get-tuple-element.191, bf16[2,2048,256]{2,1,0:T(8,128)(2,1)} %get-tuple-element.193, s32[]{:T(128)} %get-tuple-element.182, f32[512,256]{1,0:T(8,128)S(1)} %get-tuple-element.183, pred[]{:T(512)S(6)} %compare.38), kind=kOutput, calls=%fused_computation.8.clone.1 | convolution fusion | flops 538181632 | bytes 2107905 | tf_op jit(solution)/shard_map/while/body/eval_jaxpr/while/body/eval_jaxpr/dot_general | solution.py:24
  42.9 2.1 %fusion.37 = f32[512,256]{1,0:T(8,128)S(1)} fusion(s32[2048]{0:T(1024)S(1)} %bitcast.53, s32[512]{0:T(512)S(1)} %get-tuple-element.191, bf16[2,2048,256]{2,1,0:T(8,128)(2,1)} %get-tuple-element.193, s32[]{:T(128)} %get-tuple-element.182, f32[512,256]{1,0:T(8,128)S(1)} %get-tuple-element.183, pred[]{:T(512)S(6)} %compare.38), kind=kOutput, calls=%fused_computation.8.clone.1 | convolution fusion | flops 538181632 | bytes 2107905 | tf_op jit(solution)/shard_map/while/body/eval_jaxpr/while/body/eval_jaxpr/dot_general | solution.py:24
  45.0 0.7 bitcast_dynamic-update-slice_fusion.2
  45.7 3.6 %all-to-all-start.2 = ((bf16[16,64,256]{2,1,0:T(8,128)(2,1)}), bf16[16,64,256]{2,1,0:T(8,128)(2,1)S(1)}, u32[]{:S(2)}, u32[]{:S(2)}) async-start(bf16[16,64,256]{2,1,0:T(8,128)(2,1)} %bitcast.11), calls=%async_computation.2 | async-start | bytes 1048576 | tf_op jit(solution)/shard_map/all_to_all | solution.py:74
  49.3 9.5 %all-to-all-done.2 = bf16[16,64,256]{2,1,0:T(8,128)(2,1)S(1)} async-done(((bf16[16,64,256]{2,1,0:T(8,128)(2,1)}), bf16[16,64,256]{2,1,0:T(8,128)(2,1)S(1)}, u32[]{:S(2)}, u32[]{:S(2)}) %all-to-all-start.2) | async-done | bytes 524320 | tf_op jit(solution)/shard_map/all_to_all | solution.py:74
  58.8 1.9 %gather_fusion = bf16[512,256]{1,0:T(8,128)(2,1)S(1)} fusion(bf16[1024,256]{1,0:T(8,128)(2,1)S(1)} %bitcast.51, s32[1024]{0:T(1024)S(1)} %pad_clamp_fusion.1), kind=kCustom, calls=%fused_computation | custom fusion | bytes 526336 | tf_op jit(solution)/shard_map/gather | solution.py:76
  60.8 0.8 %fusion.10 = bf16[8,64,256]{2,1,0:T(8,128)(2,1)} fusion(bf16[8,64,256]{2,1,0:T(8,128)(2,1)S(1)} %bitcast.54, pred[8,64]{1,0:T(8,128)(4,1)S(1)} %compare_bitcast_fusion), kind=kLoop, calls=%fused_computation.16 | loop fusion | flops 393216 | bytes 524800 | tf_op jit(solution)/shard_map/convert_element_type | solution.py:78
  61.6 6.3 %all-to-all-start.3 = ((bf16[8,64,256]{2,1,0:T(8,128)(2,1)}), bf16[8,64,256]{2,1,0:T(8,128)(2,1)S(1)}, u32[]{:S(2)}, u32[]{:S(2)}) async-start(bf16[8,64,256]{2,1,0:T(8,128)(2,1)} %fusion.10), calls=%async_computation.3 | async-start | bytes 524288 | tf_op jit(solution)/shard_map/all_to_all | solution.py:79
  67.9 6.5 %all-to-all-done.3 = bf16[8,64,256]{2,1,0:T(8,128)(2,1)S(1)} async-done(((bf16[8,64,256]{2,1,0:T(8,128)(2,1)}), bf16[8,64,256]{2,1,0:T(8,128)(2,1)S(1)}, u32[]{:S(2)}, u32[]{:S(2)}) %all-to-all-start.3) | async-done | bytes 262176 | tf_op jit(solution)/shard_map/all_to_all | solution.py:79
  74.4 1.8 %gather_fusion.1 = bf16[256,256]{1,0:T(8,128)(2,1)} fusion(bf16[512,256]{1,0:T(8,128)(2,1)S(1)} %bitcast.52, s32[1024]{0:T(1024)S(1)} %pad_clamp_fusion), kind=kCustom, calls=%fused_computation.1 | custom fusion | bytes 263168 | tf_op jit(solution)/shard_map/gather | solution.py:82
  (34 shorter events, 1.0 us)
Async XLA Ops:
  20.9 14.1 %all-to-all-start.1 = ((s32[16,1,64]{2,1,0:T(1,128)}), s32[16,1,64]{2,1,0:T(1,128)S(1)}, u32[]{:S(2)}, u32[]{:S(2)}) async-start(s32[16,1,64]{2,1,0:T(1,128)} %all_to_all.20), calls=%async_computation.1 | async-start | bytes 16384 | tf_op jit(solution)/shard_map/all_to_all | solution.py:68
  45.7 13.1 %all-to-all-start.2 = ((bf16[16,64,256]{2,1,0:T(8,128)(2,1)}), bf16[16,64,256]{2,1,0:T(8,128)(2,1)S(1)}, u32[]{:S(2)}, u32[]{:S(2)}) async-start(bf16[16,64,256]{2,1,0:T(8,128)(2,1)} %bitcast.11), calls=%async_computation.2 | async-start | bytes 1048576 | tf_op jit(solution)/shard_map/all_to_all | solution.py:74
  61.6 12.8 %all-to-all-start.3 = ((bf16[8,64,256]{2,1,0:T(8,128)(2,1)}), bf16[8,64,256]{2,1,0:T(8,128)(2,1)S(1)}, u32[]{:S(2)}, u32[]{:S(2)}) async-start(bf16[8,64,256]{2,1,0:T(8,128)(2,1)} %fusion.10), calls=%async_computation.3 | async-start | bytes 524288 | tf_op jit(solution)/shard_map/all_to_all | solution.py:79
where the time goes:
time: 76.9 us; the launch traced here: 76.2 us
  waiting for transfers between devices  21.6 us (28%)
  starting transfers between devices  17.6 us (23%)
  local copies, waits for them, and re-layouts  12 us (16%)
  blocking collectives  10.2 us (13%)
  matrix products  8.29 us (11%)
  other arithmetic  6.2 us (8%)
    all_to_all x1, blocking collectives, on_device(): lax.all_to_all(outgoing, 'row', split_axis=0, concat_axis=0, tiled=True)  10.2 us
    all_to_all x1, waiting for transfers between devices, on_device(): lax.all_to_all(found, 'col', split_axis=0, concat_axis=0, tiled=True)  9.49 us
    dot_general x4, matrix products, add_block(): jnp.dot(matches, row_block, preferred_element_type=jnp.float32)  8.29 us
    all_to_all x1, starting transfers between devices, on_device(): lax.all_to_all(requests, 'col', split_axis=0, concat_axis=0, tiled=True)  7.77 us
    all_to_all x1, waiting for transfers between devices, on_device(): lax.all_to_all(answers, 'row', split_axis=0, concat_axis=0, tiled=True)  6.49 us
    all_to_all x1, starting transfers between devices, on_device(): lax.all_to_all(answers, 'row', split_axis=0, concat_axis=0, tiled=True)  6.29 us
    all_to_all x1, waiting for transfers between devices, on_device(): lax.all_to_all(requests, 'col', split_axis=0, concat_axis=0, tiled=True)  5.62 us
    all_to_all x1, starting transfers between devices, on_device(): lax.all_to_all(found, 'col', split_axis=0, concat_axis=0, tiled=True)  3.57 us
  transfers between devices with their start and end apart: 3, of which 3 were waited for; matrix products, arithmetic and copies ran while one was open for 1% of the time, Pallas kernels for 0%

commit v1 on v0

v1 whole, which is shorter than its diff:
```python
import functools

import jax
import jax.numpy as jnp
from jax import lax
from jax.experimental import pallas as pl
from jax.experimental.pallas import tpu as pltpu
from jax.sharding import PartitionSpec as P

MESH = pl.DeviceIdType.MESH
SLOTS = 8
ROWS = 8
COLS = 16
DEVICES = ROWS * COLS
GROUP = 32
GROUPS = DEVICES // GROUP
BLOCK = 4096
FACTS = 256
WIDTH = 256
STEP = 512


def code_of(offset):
    value = (128 + (offset & 127)).astype(jnp.float32)
    high = offset >> 7
    for bit in range(5):
        value = jnp.where(((high >> bit) & 1) == 1, value * float(2 ** (2**bit)), value)
    return value


def kernel(
    fact_ref,
    dim_ref,
    payload_ref,
    out_ref,
    table,
    codes,
    ask,
    asked,
    answer,
    got,
    place,
    copy_sem,
    ask_send,
    ask_recv,
    ans_send,
    ans_recv,
):
    row = lax.axis_index("row")
    col = lax.axis_index("col")
    me = row * COLS + col
    plane = me // GROUP
    inner = me % GROUP

    def peer(group, step):
        other = ((plane + group) % GROUPS) * GROUP + (inner + step) % GROUP
        return other, (other // COLS, other % COLS)

    barrier = pltpu.get_barrier_semaphore()
    for group in range(GROUPS):

        def greet(step, carry):
            unused, where = peer(group, step)
            pl.semaphore_signal(barrier, inc=1, device_id=where, device_id_type=MESH)
            return carry

        lax.fori_loop(1 if group == 0 else 0, GROUP, greet, 0)

    load = pltpu.make_async_copy(payload_ref, table, copy_sem)
    load.start()

    keys = jnp.concatenate([fact_ref[0:1, :], fact_ref[1:2, :]], axis=1)
    owner = keys >> 12
    code = code_of(keys & (BLOCK - 1))
    member = lax.broadcasted_iota(jnp.int32, (DEVICES, FACTS), 0) == owner
    member16 = member.astype(jnp.float32).astype(jnp.bfloat16)
    before = (
        lax.broadcasted_iota(jnp.int32, (FACTS, FACTS), 0)
        < lax.broadcasted_iota(jnp.int32, (FACTS, FACTS), 1)
    )
    before16 = before.astype(jnp.float32).astype(jnp.bfloat16)
    counts = jnp.dot(member16, before16, preferred_element_type=jnp.float32)
    rank = jnp.sum(jnp.where(member, counts, 0.0), axis=0, keepdims=True)
    coded = jnp.where(member, code, 0.0).astype(jnp.bfloat16)
    ranked = (
        lax.broadcasted_iota(jnp.int32, (DEVICES, FACTS), 0).astype(jnp.float32) == rank
    )
    ranked16 = ranked.astype(jnp.float32).astype(jnp.bfloat16)
    requests = lax.dot_general(
        coded, ranked16, (((1,), (1,)), ((), ())), preferred_element_type=jnp.float32
    )
    ask[...] = requests.reshape(DEVICES, 1, DEVICES)

    pl.semaphore_wait(barrier, DEVICES - 1)

    for group in (2, 1, 3, 0):

        def request(step, carry):
            other, where = peer(group, step)
            pltpu.make_async_remote_copy(
                src_ref=ask.at[other],
                dst_ref=asked.at[me],
                send_sem=ask_send,
                recv_sem=ask_recv.at[(GROUPS - group) % GROUPS],
                device_id=where,
                device_id_type=MESH,
            ).start()
            return carry

        lax.fori_loop(1 if group == 0 else 0, GROUP, request, 0)

    asked[me] = ask[me]

    dim_code = code_of(dim_ref[...] & (BLOCK - 1))
    for part in range(BLOCK // 128):
        codes[:, part * 128 : (part + 1) * 128] = jnp.broadcast_to(
            dim_code[part : part + 1, :], (16, 128)
        ).astype(jnp.bfloat16)

    slot_row = owner.astype(jnp.float32) * SLOTS + rank
    same = (
        lax.broadcasted_iota(jnp.int32, (FACTS, FACTS), 0)
        == lax.broadcasted_iota(jnp.int32, (FACTS, FACTS), 1)
    )
    slot = jnp.sum(jnp.where(same, slot_row, 0.0), axis=1, keepdims=True)
    slot = jnp.broadcast_to(slot, (FACTS, 128))
    lane = lax.broadcasted_iota(jnp.int32, (FACTS, 128), 1).astype(jnp.float32)
    for part in range(DEVICES * SLOTS // 128):
        place[:, part * 128 : (part + 1) * 128] = (
            (slot == lane + float(part * 128)).astype(jnp.float32).astype(jnp.bfloat16)
        )

    load.wait()

    picked = lax.broadcasted_iota(
        jnp.int32, (GROUP, SLOTS, 128), 1
    ) == lax.broadcasted_iota(jnp.int32, (GROUP, SLOTS, 128), 2)
    ones = jnp.ones((128, 128), jnp.bfloat16)
    rows = GROUP * SLOTS
    for group in (0, 1, 3, 2):
        source = (plane + group) % GROUPS
        first = source * GROUP
        count = GROUP - 1 if group == 0 else GROUP
        arrived = asked.at[pl.ds(0, count)]
        pltpu.make_async_copy(arrived, arrived, ask_recv.at[group]).wait()
        block = asked[pl.ds(first, GROUP)]
        spread = jnp.where(picked, jnp.broadcast_to(block, (GROUP, SLOTS, 128)), 0.0)
        spread = spread.reshape(rows, 128).astype(jnp.bfloat16)
        query = jnp.dot(spread, ones, preferred_element_type=jnp.float32).astype(jnp.bfloat16)
        wide = jnp.concatenate([query] * (STEP // 128), axis=1)
        total = jnp.zeros((rows, WIDTH), jnp.float32)
        for part in range(BLOCK // STEP):
            code_row = codes[:, part * STEP : (part + 1) * STEP]
            hit = jnp.concatenate([code_row] * (rows // 16), axis=0) == wide
            hit = jnp.where(hit, jnp.bfloat16(1), jnp.bfloat16(0))
            total = total + jnp.dot(
                hit,
                table[part * STEP : (part + 1) * STEP, :],
                preferred_element_type=jnp.float32,
            )
        answer[pl.ds(first, GROUP)] = total.astype(jnp.bfloat16).reshape(GROUP, SLOTS, WIDTH)

        def reply(step, carry):
            other, where = peer(group, step)
            pltpu.make_async_remote_copy(
                src_ref=answer.at[other],
                dst_ref=got.at[me],
                send_sem=ans_send,
                recv_sem=ans_recv,
                device_id=where,
                device_id_type=MESH,
            ).start()
            return carry

        lax.fori_loop(1 if group == 0 else 0, GROUP, reply, 0)
        if group == 0:
            got[me] = answer[me]

    landed = got.at[pl.ds(0, DEVICES - 1)]
    pltpu.make_async_copy(landed, landed, ans_recv).wait()
    fetched = got[...].reshape(DEVICES * SLOTS, WIDTH)
    out_ref[...] = jnp.dot(
        place[...], fetched, preferred_element_type=jnp.float32
    ).astype(jnp.bfloat16)

    sent = ask.at[pl.ds(0, DEVICES - 1)]
    pltpu.make_async_copy(sent, sent, ask_send).wait()
    pltpu.make_async_copy(landed, landed, ans_send).wait()


def on_device(fact_keys, dim_keys, dim_payload):
    vmem = pl.BlockSpec(memory_space=pltpu.VMEM)
    return pl.pallas_call(
        kernel,
        out_shape=jax.ShapeDtypeStruct((FACTS, WIDTH), jnp.bfloat16),
        in_specs=[vmem, vmem, pl.BlockSpec(memory_space=pl.ANY)],
        out_specs=vmem,
        scratch_shapes=[
            pltpu.VMEM((BLOCK, WIDTH), jnp.bfloat16),
            pltpu.VMEM((16, BLOCK), jnp.bfloat16),
            pltpu.VMEM((DEVICES, 1, 128), jnp.float32),
            pltpu.VMEM((DEVICES, 1, 128), jnp.float32),
            pltpu.VMEM((DEVICES, SLOTS, WIDTH), jnp.bfloat16),
            pltpu.VMEM((DEVICES, SLOTS, WIDTH), jnp.bfloat16),
            pltpu.VMEM((FACTS, DEVICES * SLOTS), jnp.bfloat16),
            pltpu.SemaphoreType.DMA,
            pltpu.SemaphoreType.DMA,
            pltpu.SemaphoreType.DMA((GROUPS,)),
            pltpu.SemaphoreType.DMA,
            pltpu.SemaphoreType.DMA,
        ],
        compiler_params=pltpu.CompilerParams(collective_id=0, has_side_effects=True),
    )(fact_keys.reshape(2, 128), dim_keys.reshape(BLOCK // 128, 128), dim_payload)


def solution(mesh):
    return jax.shard_map(
        on_device,
        mesh=mesh,
        in_specs=(P(("row", "col")), P(("row", "col")), P(("row", "col"), None)),
        out_specs=P(("row", "col"), None),
        check_vma=False,
    )
```

time: 76.9 us -> 36.1 us (0.47)
  Pallas kernels: 0 us -> 34.2 us
  waiting for transfers between devices: 21.6 us -> 0 us
  starting transfers between devices: 17.6 us -> 0 us
  local copies, waits for them, and re-layouts: 12 us -> 1.57 us
  blocking collectives: 10.2 us -> 0 us
  matrix products: 8.29 us -> 0 us
  other arithmetic: 6.2 us -> 0 us
    pallas_call x0 -> x1, Pallas kernels: none -> 34.2 us  [on_device(): pl.pallas_call(kernel, out_shape=jax.ShapeDtypeStruct((FACTS, WIDTH), jnp...]
    all_to_all x3 -> x0, waiting for transfers between devices: 21.6 us -> none  [the longest x1 9.49 us: on_device(): lax.all_to_all(found, 'col', split_axis=0, concat_axis=0, tiled=True)]
    all_to_all x3 -> x0, starting transfers between devices: 17.6 us -> none  [the longest x1 7.77 us: on_device(): lax.all_to_all(requests, 'col', split_axis=0, concat_axis=0, tiled=True)]
    all_to_all x1 -> x0, blocking collectives: 10.2 us -> none  [on_device(): lax.all_to_all(outgoing, 'row', split_axis=0, concat_axis=0, tiled=True)]
    dot_general x4 -> x0, matrix products: 8.29 us -> none  [add_block(): jnp.dot(matches, row_block, preferred_element_type=jnp.float32)]
    scatter x2 -> x0, local copies, waits for them, and re-layouts: 4 us -> none  [the longest x1 2.45 us: on_device(): jnp.full((col_devices * slots + 1,), -1, jnp.int32).at[target].set(incoming)]
    gather x2 -> x0, local copies, waits for them, and re-layouts: 3.75 us -> none  [the longest x1 1.95 us: on_device(): fetched = flat_rows[jnp.where(valid, target, 0)]]
    another operation x4 -> x0, other arithmetic: 1.81 us -> none
  transfers between devices with their start and end apart: 3 -> 0, of which waited for: 3 -> 0; matrix products, arithmetic and copies ran while one was open for 1% -> 0% of each run, Pallas kernels for 0% -> 0%
where the time goes in v1:
time: 36.1 us; the launch traced here: 35.7 us
  Pallas kernels  34.2 us (95%)
  local copies, waits for them, and re-layouts  1.57 us (4%)
    pallas_call x1, Pallas kernels, on_device(): pl.pallas_call(kernel, out_shape=jax.ShapeDtypeStruct((FACTS, WIDTH), jnp...  34.2 us
    unnamed x1, local copies, waits for them, and re-layouts  1.57 us

profile of v1, /device:TPU:1, one launch (start us, length us, event | category | flops | bytes accessed | tf_op | source)
XLA Modules:
  0.0 35.7 jit_solution(11608089853558570338)
XLA Ops:
  0.0 34.2 %shard_map.37 = bf16[256,256]{1,0:T(8,128)(2,1)} custom-call(s32[2,128]{1,0:T(2,128)} %bitcast.3, s32[32,128]{1,0:T(8,128)} %bitcast.2, bf16[4096,256]{1,0:T(8,128)(2,1)} %payload_ref.1), custom_call_target="tpu_custom_call" | custom-call | tf_op jit(solution)/shard_map/pallas_call | solution.py:193
  34.2 1.6 %copy.5 = bf16[256,256]{1,0:T(8,128)(2,1)} copy(bf16[256,256]{1,0:T(8,128)(2,1)} %shard_map.37) | data formatting | bytes 262144

commit v2 on v1

v2 whole, which is shorter than its diff:
```python
import jax
import jax.numpy as jnp
from jax import lax
from jax.experimental import pallas as pl
from jax.experimental.pallas import tpu as pltpu
from jax.sharding import PartitionSpec as P

MESH = pl.DeviceIdType.MESH
SLOTS = 8
ROWS = 8
COLS = 16
DEVICES = ROWS * COLS
PLANE = 4
BLOCK = 4096
FACTS = 256
WIDTH = 256
STEP = 512
ORDER = (0, 1, 3, 2)


def code_of(offset):
    high = offset >> 7
    scaled = ((128 + (offset & 127)) << (high & 15)).astype(jnp.float32)
    return scaled * jnp.where(high >= 16, 65536.0, 1.0)


def iota(shape, axis):
    return lax.broadcasted_iota(jnp.int32, shape, axis)


def bits(mask):
    return mask.astype(jnp.float32).astype(jnp.bfloat16)


def kernel(
    fact_hbm,
    dim_hbm,
    payload_ref,
    out_ref,
    facts,
    dims,
    table,
    codes,
    keys_at,
    tags,
    coded_at,
    answer,
    got,
    place,
    copy_sem,
    key_send,
    line_recv,
    plane_recv,
    ans_send,
    ans_recv,
):
    row = lax.axis_index("row")
    col = lax.axis_index("col")
    me = row * COLS + col
    depth = col // PLANE
    other_rows = [lax.rem(row + step, ROWS) for step in range(1, ROWS)]
    other_cols = {}
    for far in range(PLANE):
        layer = lax.rem(depth + far, PLANE)
        for near in range(PLANE):
            other_cols[far, near] = layer * PLANE + lax.rem(col + near, PLANE)

    load_facts = pltpu.make_async_copy(fact_hbm, facts, copy_sem.at[0])
    load_facts.start()
    barrier = pltpu.get_barrier_semaphore()
    for other in other_rows:
        pl.semaphore_signal(barrier, inc=1, device_id=(other, col), device_id_type=MESH)
    for far in range(PLANE):
        for near in range(PLANE):
            if far or near:
                pl.semaphore_signal(
                    barrier,
                    inc=1,
                    device_id=(row, other_cols[far, near]),
                    device_id_type=MESH,
                )
    load_dims = pltpu.make_async_copy(dim_hbm, dims, copy_sem.at[1])
    load_dims.start()
    load_table = pltpu.make_async_copy(payload_ref, table, copy_sem.at[2])
    load_table.start()
    load_facts.wait()

    keys = jnp.concatenate([facts[0:1, :], facts[1:2, :]], axis=1)
    owner = keys >> 12
    member = iota((DEVICES, FACTS), 0) == owner
    before = bits(iota((FACTS, FACTS), 0) < iota((FACTS, FACTS), 1))
    counts = jnp.dot(bits(member), before, preferred_element_type=jnp.float32)
    rank = jnp.sum(jnp.where(member, counts, 0.0), axis=0, keepdims=True)
    slot_row = owner * SLOTS + rank.astype(jnp.int32)
    packed = slot_row * BLOCK + (keys & (BLOCK - 1))
    mine = keys_at.at[col, row]
    mine[0:1, :] = packed[:, :128]
    mine[1:2, :] = packed[:, 128:]

    pl.semaphore_wait(barrier, ROWS + COLS - 2)

    for other in other_rows:
        pltpu.make_async_remote_copy(
            src_ref=mine,
            dst_ref=mine,
            send_sem=key_send.at[0],
            recv_sem=line_recv,
            device_id=(other, col),
            device_id_type=MESH,
        ).start()

    same = iota((FACTS, FACTS), 0) == iota((FACTS, FACTS), 1)
    slot = jnp.sum(
        jnp.where(same, slot_row.astype(jnp.float32), 0.0), axis=1, keepdims=True
    )
    slot = jnp.broadcast_to(slot, (FACTS, 128))
    lane = iota((FACTS, 128), 1).astype(jnp.float32)
    for part in range(DEVICES * SLOTS // 128):
        place[:, part * 128 : (part + 1) * 128] = bits(slot == lane + float(part * 128))

    line = keys_at.at[0, pl.ds(0, ROWS - 1)]
    pltpu.make_async_copy(line, line, line_recv).wait()

    for far in (2, 1, 3, 0):
        for near in (2, 1, 3, 0):
            if far or near:
                pltpu.make_async_remote_copy(
                    src_ref=keys_at.at[col],
                    dst_ref=keys_at.at[col],
                    send_sem=key_send.at[1],
                    recv_sem=plane_recv.at[(PLANE - far) % PLANE],
                    device_id=(row, other_cols[far, near]),
                    device_id_type=MESH,
                ).start()

    load_dims.wait()
    dim_code = code_of(dims[...] & (BLOCK - 1))
    for part in range(BLOCK // 128):
        codes[:, part * 128 : (part + 1) * 128] = jnp.broadcast_to(
            dim_code[part : part + 1, :], (16, 128)
        ).astype(jnp.bfloat16)
    load_table.wait()

    ones = jnp.ones((FACTS, 128), jnp.bfloat16)
    count = PLANE * ROWS
    rows = count * SLOTS
    wanted = me * SLOTS + iota((count, SLOTS, 128), 1)
    for far in ORDER:
        layer = lax.rem(depth + far, PLANE)
        arrived = keys_at.at[pl.ds(0, PLANE if far else PLANE - 1)]
        pltpu.make_async_copy(arrived, arrived, plane_recv.at[far]).wait()
        block = keys_at[pl.ds(layer * PLANE, PLANE)].reshape(count, 2, 128)
        tags[...] = block >> 12
        coded_at[...] = code_of(block & (BLOCK - 1))
        spread = []
        for half in range(2):
            tag = jnp.broadcast_to(tags[:, half : half + 1, :], (count, SLOTS, 128))
            code = jnp.broadcast_to(coded_at[:, half : half + 1, :], (count, SLOTS, 128))
            spread.append(
                jnp.where(tag == wanted, code, 0.0).reshape(rows, 128).astype(jnp.bfloat16)
            )
        query = jnp.dot(
            jnp.concatenate(spread, axis=1), ones, preferred_element_type=jnp.float32
        ).astype(jnp.bfloat16)
        wide = jnp.concatenate([query] * (STEP // 128), axis=1)
        total = jnp.zeros((rows, WIDTH), jnp.float32)
        for part in range(BLOCK // STEP):
            code_row = codes[:, part * STEP : (part + 1) * STEP]
            hit = jnp.concatenate([code_row] * (rows // 16), axis=0) == wide
            hit = jnp.where(hit, jnp.bfloat16(1), jnp.bfloat16(0))
            total = total + jnp.dot(
                hit,
                table[part * STEP : (part + 1) * STEP, :],
                preferred_element_type=jnp.float32,
            )
        answer[far * count : (far + 1) * count] = total.astype(jnp.bfloat16).reshape(
            count, SLOTS, WIDTH
        )
        for near in range(PLANE):
            there = layer * PLANE + near
            for other in range(ROWS):

                def reply(there=there, near=near, other=other, far=far):
                    pltpu.make_async_remote_copy(
                        src_ref=answer.at[far * count + near * ROWS + other],
                        dst_ref=got.at[me],
                        send_sem=ans_send,
                        recv_sem=ans_recv,
                        device_id=(other, there),
                        device_id_type=MESH,
                    ).start()

                if far:
                    reply()
                else:
                    pl.when(jnp.logical_or(other != row, there != col))(reply)

        if far == 0:
            got[me] = answer[lax.rem(col, PLANE) * ROWS + row]

    landed = got.at[pl.ds(0, DEVICES - 1)]
    pltpu.make_async_copy(landed, landed, ans_recv).wait()
    out_ref[...] = jnp.dot(
        place[...],
        got[...].reshape(DEVICES * SLOTS, WIDTH),
        preferred_element_type=jnp.float32,
    ).astype(jnp.bfloat16)

    pltpu.make_async_copy(line, line, key_send.at[0]).wait()
    sent = keys_at.at[pl.ds(0, COLS - 1)]
    pltpu.make_async_copy(sent, sent, key_send.at[1]).wait()
    pltpu.make_async_copy(landed, landed, ans_send).wait()


def on_device(fact_keys, dim_keys, dim_payload):
    whole = pl.BlockSpec(memory_space=pl.ANY)
    count = PLANE * ROWS
    return pl.pallas_call(
        kernel,
        out_shape=jax.ShapeDtypeStruct((FACTS, WIDTH), jnp.bfloat16),
        in_specs=[whole, whole, whole],
        out_specs=pl.BlockSpec(memory_space=pltpu.VMEM),
        scratch_shapes=[
            pltpu.VMEM((2, 128), jnp.int32),
            pltpu.VMEM((BLOCK // 128, 128), jnp.int32),
            pltpu.VMEM((BLOCK, WIDTH), jnp.bfloat16),
            pltpu.VMEM((16, BLOCK), jnp.bfloat16),
            pltpu.VMEM((COLS, ROWS, 2, 128), jnp.int32),
            pltpu.VMEM((count, 2, 128), jnp.int32),
            pltpu.VMEM((count, 2, 128), jnp.float32),
            pltpu.VMEM((DEVICES, SLOTS, WIDTH), jnp.bfloat16),
            pltpu.VMEM((DEVICES, SLOTS, WIDTH), jnp.bfloat16),
            pltpu.VMEM((FACTS, DEVICES * SLOTS), jnp.bfloat16),
            pltpu.SemaphoreType.DMA((3,)),
            pltpu.SemaphoreType.DMA((2,)),
            pltpu.SemaphoreType.DMA,
            pltpu.SemaphoreType.DMA((PLANE,)),
            pltpu.SemaphoreType.DMA,
            pltpu.SemaphoreType.DMA,
        ],
        compiler_params=pltpu.CompilerParams(collective_id=0, has_side_effects=True),
    )(fact_keys.reshape(2, 128), dim_keys.reshape(BLOCK // 128, 128), dim_payload)


def solution(mesh):
    return jax.shard_map(
        on_device,
        mesh=mesh,
        in_specs=(P(("row", "col")), P(("row", "col")), P(("row", "col"), None)),
        out_specs=P(("row", "col"), None),
        check_vma=False,
    )
```

time: 36.1 us -> 30.2 us (0.84)
  Pallas kernels: 34.2 us -> 28.5 us
    pallas_call x1, Pallas kernels: 34.2 us -> 28.5 us  [on_device(): pl.pallas_call(kernel, out_shape=jax.ShapeDtypeStruct((FACTS, WIDTH), jnp...]
where the time goes in v2:
time: 30.2 us; the launch traced here: 30.1 us
  Pallas kernels  28.5 us (94%)
  local copies, waits for them, and re-layouts  1.57 us (5%)
    pallas_call x1, Pallas kernels, on_device(): pl.pallas_call(kernel, out_shape=jax.ShapeDtypeStruct((FACTS, WIDTH), jnp...  28.5 us
    unnamed x1, local copies, waits for them, and re-layouts  1.57 us

profile of v2, /device:TPU:1, one launch (start us, length us, event | category | flops | bytes accessed | tf_op | source)
XLA Modules:
  0.0 30.1 jit_solution(7497927528196545606)
XLA Ops:
  0.0 28.5 %shard_map.37 = bf16[256,256]{1,0:T(8,128)(2,1)} custom-call(s32[2,128]{1,0:T(2,128)} %bitcast.3, s32[32,128]{1,0:T(8,128)} %bitcast.2, bf16[4096,256]{1,0:T(8,128)(2,1)} %payload_ref.1), custom_call_target="tpu_custom_call" | custom-call | tf_op jit(solution)/shard_map/pallas_call | solution.py:218
  28.5 1.6 %copy.5 = bf16[256,256]{1,0:T(8,128)(2,1)} copy(bf16[256,256]{1,0:T(8,128)(2,1)} %shard_map.37) | data formatting | bytes 262144

commit v3 on v2

v3 whole, which is shorter than its diff:
```python
import jax
import jax.numpy as jnp
from jax import lax
from jax.experimental import pallas as pl
from jax.experimental.pallas import tpu as pltpu
from jax.sharding import PartitionSpec as P

MESH = pl.DeviceIdType.MESH
SLOTS = 8
ROWS = 8
COLS = 16
PLANES = 4
CORES = 2
DEVICES = ROWS * COLS
BLOCK = 4096
FACTS = 256
WIDTH = 256
STEP = 512
COUNT = CORES * COLS


def code_of(offset):
    high = offset >> 7
    scaled = ((128 + (offset & 127)) << (high & 15)).astype(jnp.float32)
    return scaled * jnp.where(high >= 16, 65536.0, 1.0)


def iota(shape, axis):
    return lax.broadcasted_iota(jnp.int32, shape, axis)


def bits(mask):
    return mask.astype(jnp.float32).astype(jnp.bfloat16)


def kernel(
    fact_hbm,
    dim_hbm,
    payload_ref,
    out_ref,
    facts,
    dims,
    table,
    codes,
    ask,
    asked,
    answer,
    got,
    place,
    copy_sem,
    key_send,
    plane_recv,
    line_recv,
    ans_send,
    ans_recv,
):
    row = lax.axis_index("row")
    col = lax.axis_index("col")
    me = row * COLS + col
    plane = row // CORES
    other_rows = [lax.rem(row + step, ROWS) for step in range(1, ROWS)]
    depth = col // 4
    other_cols = [
        lax.rem(depth + far, 4) * 4 + lax.rem(col + near, 4)
        for far in (2, 1, 3, 0)
        for near in (2, 1, 3, 0)
        if far or near
    ]

    load_facts = pltpu.make_async_copy(fact_hbm, facts, copy_sem.at[0])
    load_facts.start()
    barrier = pltpu.get_barrier_semaphore()
    for other in other_cols:
        pl.semaphore_signal(barrier, inc=1, device_id=(row, other), device_id_type=MESH)
    for other in other_rows:
        pl.semaphore_signal(barrier, inc=1, device_id=(other, col), device_id_type=MESH)
    load_dims = pltpu.make_async_copy(dim_hbm, dims, copy_sem.at[1])
    load_dims.start()
    load_table = pltpu.make_async_copy(payload_ref, table, copy_sem.at[2])
    load_table.start()
    load_facts.wait()

    keys = jnp.concatenate([facts[0:1, :], facts[1:2, :]], axis=1)
    owner = keys >> 12
    member = iota((DEVICES, FACTS), 0) == owner
    before = bits(iota((FACTS, FACTS), 0) < iota((FACTS, FACTS), 1))
    counts = jnp.dot(bits(member), before, preferred_element_type=jnp.float32)
    rank = jnp.sum(jnp.where(member, counts, 0.0), axis=0, keepdims=True).astype(jnp.int32)
    code = code_of(keys & (BLOCK - 1))
    by_col = jnp.where(iota((COLS, FACTS), 0) == (owner & (COLS - 1)), code, 0.0)
    by_slot = iota((128, FACTS), 0) == (owner >> 4) * SLOTS + rank
    requests = lax.dot_general(
        by_col.astype(jnp.bfloat16),
        bits(by_slot),
        (((1,), (1,)), ((), ())),
        preferred_element_type=jnp.float32,
    )
    ask[...] = requests.reshape(COLS, 1, 128)
    asked[row, col] = ask[col]

    pl.semaphore_wait(barrier, ROWS + COLS - 2)

    for other in other_cols:
        pltpu.make_async_remote_copy(
            src_ref=ask.at[other],
            dst_ref=asked.at[row, col],
            send_sem=key_send.at[0],
            recv_sem=plane_recv,
            device_id=(row, other),
            device_id_type=MESH,
        ).start()

    slot_row = owner * SLOTS + rank
    same = iota((FACTS, FACTS), 0) == iota((FACTS, FACTS), 1)
    slot = jnp.sum(
        jnp.where(same, slot_row.astype(jnp.float32), 0.0), axis=1, keepdims=True
    )
    slot = jnp.broadcast_to(slot, (FACTS, 128))
    lane = iota((FACTS, 128), 1).astype(jnp.float32)
    for part in range(DEVICES * SLOTS // 128):
        place[:, part * 128 : (part + 1) * 128] = bits(slot == lane + float(part * 128))
    load_dims.wait()
    dim_code = code_of(dims[...] & (BLOCK - 1))
    for part in range(BLOCK // 128):
        codes[:, part * 128 : (part + 1) * 128] = jnp.broadcast_to(
            dim_code[part : part + 1, :], (16, 128)
        ).astype(jnp.bfloat16)
    load_table.wait()

    sheet = asked.at[0, pl.ds(0, COLS - 1)]
    pltpu.make_async_copy(sheet, sheet, plane_recv).wait()

    for other in other_rows:
        pltpu.make_async_remote_copy(
            src_ref=asked.at[row],
            dst_ref=asked.at[row],
            send_sem=key_send.at[1],
            recv_sem=line_recv.at[row],
            device_id=(other, col),
            device_id_type=MESH,
        ).start()

    picked = iota((COUNT, SLOTS, 128), 2) == row * SLOTS + iota((COUNT, SLOTS, 128), 1)
    ones = jnp.ones((128, 128), jnp.bfloat16)
    rows = COUNT * SLOTS
    turns = [0, 1, 2, 3]

    def wait_for(turn):
        for core in range(CORES):
            source = turns[turn] * CORES + core

            def arrive(source=source):
                block = asked.at[0]
                pltpu.make_async_copy(block, block, line_recv.at[source]).wait()

            if True:
                pl.when(source != row)(arrive)
            else:
                arrive()

    def queries(turn):
        block = asked[pl.ds(turns[turn] * CORES, CORES)].reshape(COUNT, 1, 128)
        spread = jnp.where(picked, jnp.broadcast_to(block, (COUNT, SLOTS, 128)), 0.0)
        return jnp.dot(
            spread.reshape(rows, 128).astype(jnp.bfloat16),
            ones,
            preferred_element_type=jnp.float32,
        ).astype(jnp.bfloat16)

    def lookup(query):
        parts = []
        for half in range(2):
            wide = jnp.concatenate(
                [query[half * (rows // 2) : (half + 1) * (rows // 2)]] * (STEP // 128), axis=1
            )
            total = jnp.zeros((rows // 2, WIDTH), jnp.float32)
            for part in range(BLOCK // STEP):
                code_row = codes[:, part * STEP : (part + 1) * STEP]
                hit = jnp.concatenate([code_row] * (rows // 32), axis=0) == wide
                hit = jnp.where(hit, jnp.bfloat16(1), jnp.bfloat16(0))
                total = total + jnp.dot(
                    hit,
                    table[part * STEP : (part + 1) * STEP, :],
                    preferred_element_type=jnp.float32,
                )
            parts.append(total)
        return jnp.concatenate(parts, axis=0).astype(jnp.bfloat16)

    wait_for(0)
    ahead = queries(0)
    for turn in range(PLANES):
        query = ahead
        if turn + 1 < PLANES:
            wait_for(turn + 1)
            ahead = queries(turn + 1)
        else:
            pass
        answer[turn] = lookup(query).reshape(CORES, COLS, SLOTS, WIDTH)
        for there in range(COLS):
            for core in range(CORES):
                other = turns[turn] * CORES + core

                def reply(there=there, core=core, other=other, turn=turn):
                    pltpu.make_async_remote_copy(
                        src_ref=answer.at[turn, core, there],
                        dst_ref=got.at[me],
                        send_sem=ans_send,
                        recv_sem=ans_recv,
                        device_id=(other, there),
                        device_id_type=MESH,
                    ).start()

                if True:
                    pl.when(jnp.logical_or(other != row, there != col))(reply)
                else:
                    reply()

    got[me] = answer[plane, row % CORES, col]

    landed = got.at[pl.ds(0, DEVICES - 1)]
    pltpu.make_async_copy(landed, landed, ans_recv).wait()
    out_ref[...] = jnp.dot(
        place[...],
        got[...].reshape(DEVICES * SLOTS, WIDTH),
        preferred_element_type=jnp.float32,
    ).astype(jnp.bfloat16)

    pltpu.make_async_copy(sheet, sheet, key_send.at[0]).wait()
    sent = asked.at[pl.ds(0, ROWS - 1)]
    pltpu.make_async_copy(sent, sent, key_send.at[1]).wait()
    pltpu.make_async_copy(landed, landed, ans_send).wait()


def on_device(fact_keys, dim_keys, dim_payload):
    whole = pl.BlockSpec(memory_space=pl.ANY)
    return pl.pallas_call(
        kernel,
        out_shape=pltpu.VMEM((FACTS, WIDTH), jnp.bfloat16),
        in_specs=[whole, whole, whole],
        out_specs=pl.BlockSpec(memory_space=pltpu.VMEM),
        scratch_shapes=[
            pltpu.VMEM((2, 128), jnp.int32),
            pltpu.VMEM((BLOCK // 128, 128), jnp.int32),
            pltpu.VMEM((BLOCK, WIDTH), jnp.bfloat16),
            pltpu.VMEM((16, BLOCK), jnp.bfloat16),
            pltpu.VMEM((COLS, 1, 128), jnp.float32),
            pltpu.VMEM((ROWS, COLS, 1, 128), jnp.float32),
            pltpu.VMEM((PLANES, CORES, COLS, SLOTS, WIDTH), jnp.bfloat16),
            pltpu.VMEM((DEVICES, SLOTS, WIDTH), jnp.bfloat16),
            pltpu.VMEM((FACTS, DEVICES * SLOTS), jnp.bfloat16),
            pltpu.SemaphoreType.DMA((3,)),
            pltpu.SemaphoreType.DMA((2,)),
            pltpu.SemaphoreType.DMA,
            pltpu.SemaphoreType.DMA((ROWS,)),
            pltpu.SemaphoreType.DMA,
            pltpu.SemaphoreType.DMA,
        ],
        compiler_params=pltpu.CompilerParams(collective_id=0, has_side_effects=True),
    )(fact_keys.reshape(2, 128), dim_keys.reshape(BLOCK // 128, 128), dim_payload)


def solution(mesh):
    return jax.shard_map(
        on_device,
        mesh=mesh,
        in_specs=(P(("row", "col")), P(("row", "col")), P(("row", "col"), None)),
        out_specs=P(("row", "col"), None),
        check_vma=False,
    )
```

time: 30.2 us -> 26.3 us (0.87)
  the two profiles are of different devices: /device:TPU:1 before, /device:TPU:7 now
where the time goes in v3:
time: 26.3 us; the launch traced here: 26.2 us
  Pallas kernels  25.5 us (97%)
  local copies, waits for them, and re-layouts  0.66 us (3%)
    pallas_call x1, Pallas kernels, on_device(): pl.pallas_call(kernel, out_shape=pltpu.VMEM((FACTS, WIDTH), jnp.bfloat16)...  25.5 us
    unnamed x1, local copies, waits for them, and re-layouts  0.66 us

profile of v3, /device:TPU:7, one launch (start us, length us, event | category | flops | bytes accessed | tf_op | source)
XLA Modules:
  0.0 26.2 jit_solution(5216000292521405629)
XLA Ops:
  0.0 25.5 %shard_map.37 = bf16[256,256]{1,0:T(8,128)(2,1)S(1)} custom-call(s32[2,128]{1,0:T(2,128)} %bitcast.3, s32[32,128]{1,0:T(8,128)} %bitcast.2, bf16[4096,256]{1,0:T(8,128)(2,1)} %payload_ref.1), custom_call_target="tpu_custom_call" | custom-call | tf_op jit(solution)/shard_map/pallas_call | solution.py:236
  25.6 0.7 %copy.5 = bf16[256,256]{1,0:T(8,128)(2,1)} copy(bf16[256,256]{1,0:T(8,128)(2,1)S(1)} %shard_map.37) | data formatting | bytes 262144

commit v4 on v3

v4 whole, which is shorter than its diff:
```python
import jax
import jax.numpy as jnp
from jax import lax
from jax.experimental import pallas as pl
from jax.experimental.pallas import tpu as pltpu
from jax.sharding import PartitionSpec as P

MESH = pl.DeviceIdType.MESH
SLOTS = 8
ROWS = 8
COLS = 16
SIDE = 4
PLANES = 4
CORES = 2
LINES = PLANES * CORES
SPOTS = SIDE * SIDE
DEVICES = ROWS * COLS
BLOCK = 4096
FACTS = 256
WIDTH = 256
STEP = 512
COUNT = CORES * SPOTS


def code_of(offset):
    high = offset >> 7
    scaled = ((128 + (offset & 127)) << (high & 15)).astype(jnp.float32)
    return scaled * jnp.where(high >= 16, 65536.0, 1.0)


def iota(shape, axis):
    return lax.broadcasted_iota(jnp.int32, shape, axis)


def bits(mask):
    return mask.astype(jnp.float32).astype(jnp.bfloat16)


def kernel(
    fact_hbm,
    dim_hbm,
    payload_ref,
    out_ref,
    facts,
    dims,
    table,
    codes,
    ask,
    asked,
    answer,
    got,
    place,
    copy_sem,
    key_send,
    key_recv,
    ans_send,
    ans_recv,
):
    row = lax.axis_index("row")
    col = lax.axis_index("col")
    me = row * COLS + col
    x, core = row // CORES, lax.rem(row, CORES)
    z, y = col // SIDE, lax.rem(col, SIDE)
    line, spot = z * CORES + core, x * SIDE + y
    plane = z

    def device(line, spot):
        return (
            spot // SIDE * CORES + line % CORES,
            line // CORES * SIDE + spot % SIDE,
        )

    load_facts = pltpu.make_async_copy(fact_hbm, facts, copy_sem.at[0])
    load_facts.start()
    barrier = pltpu.get_barrier_semaphore()
    for other in range(LINES):
        for there in range(SPOTS):

            def greet(other=other, there=there):
                pl.semaphore_signal(
                    barrier, inc=1, device_id=device(other, there), device_id_type=MESH
                )

            pl.when(jnp.logical_or(other != line, there != spot))(greet)
    load_dims = pltpu.make_async_copy(dim_hbm, dims, copy_sem.at[1])
    load_dims.start()
    load_table = pltpu.make_async_copy(payload_ref, table, copy_sem.at[2])
    load_table.start()
    load_facts.wait()

    keys = jnp.concatenate([facts[0:1, :], facts[1:2, :]], axis=1)
    owner = keys >> 12
    target = (((owner >> 2) & 3) * 2 + ((owner >> 4) & 1)) * SPOTS + (owner >> 5) * SIDE + (owner & 3)
    member = iota((DEVICES, FACTS), 0) == target
    before = bits(iota((FACTS, FACTS), 0) < iota((FACTS, FACTS), 1))
    counts = jnp.dot(bits(member), before, preferred_element_type=jnp.float32)
    rank = jnp.sum(jnp.where(member, counts, 0.0), axis=0, keepdims=True).astype(jnp.int32)
    code = code_of(keys & (BLOCK - 1))
    requests = lax.dot_general(
        jnp.where(member, code, 0.0).astype(jnp.bfloat16),
        bits(iota((128, FACTS), 0) == rank),
        (((1,), (1,)), ((), ())),
        preferred_element_type=jnp.float32,
    )
    ask[...] = requests.reshape(DEVICES, 1, 128)
    asked[line, spot] = ask[line * SPOTS + spot]

    pl.semaphore_wait(barrier, DEVICES - 1)

    for other in range(LINES):
        for there in range(SPOTS):

            def request(other=other, there=there):
                pltpu.make_async_remote_copy(
                    src_ref=ask.at[other * SPOTS + there],
                    dst_ref=asked.at[line, spot],
                    send_sem=key_send,
                    recv_sem=key_recv.at[plane],
                    device_id=device(other, there),
                    device_id_type=MESH,
                ).start()

            pl.when(jnp.logical_or(other != line, there != spot))(request)

    slot_row = owner * SLOTS + rank
    same = iota((FACTS, FACTS), 0) == iota((FACTS, FACTS), 1)
    slot = jnp.sum(
        jnp.where(same, slot_row.astype(jnp.float32), 0.0), axis=1, keepdims=True
    )
    slot = jnp.broadcast_to(slot, (FACTS, 128))
    lane = iota((FACTS, 128), 1).astype(jnp.float32)
    for part in range(DEVICES * SLOTS // 128):
        place[:, part * 128 : (part + 1) * 128] = bits(slot == lane + float(part * 128))
    load_dims.wait()
    dim_code = code_of(dims[...] & (BLOCK - 1))
    for part in range(BLOCK // 128):
        codes[:, part * 128 : (part + 1) * 128] = jnp.broadcast_to(
            dim_code[part : part + 1, :], (16, 128)
        ).astype(jnp.bfloat16)
    load_table.wait()

    picked = iota((COUNT, SLOTS, 128), 2) == iota((COUNT, SLOTS, 128), 1)
    ones = jnp.ones((128, 128), jnp.bfloat16)
    rows = COUNT * SLOTS
    turns = [0, 1, 2, 3]

    def wait_for(turn):
        def arrive(count):
            block = ask.at[pl.ds(0, count)]
            pltpu.make_async_copy(block, block, key_recv.at[turns[turn]]).wait()


        pl.when(plane == turns[turn])(lambda: arrive(COUNT - 1))
        pl.when(plane != turns[turn])(lambda: arrive(COUNT))

    def queries(turn):
        block = asked[pl.ds(turns[turn] * CORES, CORES)].reshape(COUNT, 1, 128)
        spread = jnp.where(picked, jnp.broadcast_to(block, (COUNT, SLOTS, 128)), 0.0)
        return jnp.dot(
            spread.reshape(rows, 128).astype(jnp.bfloat16),
            ones,
            preferred_element_type=jnp.float32,
        ).astype(jnp.bfloat16)

    def lookup(query):
        parts = []
        for half in range(2):
            wide = jnp.concatenate(
                [query[half * (rows // 2) : (half + 1) * (rows // 2)]] * (STEP // 128), axis=1
            )
            total = jnp.zeros((rows // 2, WIDTH), jnp.float32)
            for part in range(BLOCK // STEP):
                code_row = codes[:, part * STEP : (part + 1) * STEP]
                hit = jnp.concatenate([code_row] * (rows // 32), axis=0) == wide
                hit = jnp.where(hit, jnp.bfloat16(1), jnp.bfloat16(0))
                total = total + jnp.dot(
                    hit,
                    table[part * STEP : (part + 1) * STEP, :],
                    preferred_element_type=jnp.float32,
                )
            parts.append(total)
        return jnp.concatenate(parts, axis=0).astype(jnp.bfloat16)

    ahead = None
    for turn in range(PLANES):
        if ahead is None:
            wait_for(turn)
            query = queries(turn)
        else:
            query = ahead
        ahead = None
        if 1 <= turn < PLANES - 1:
            wait_for(turn + 1)
            ahead = queries(turn + 1)
        else:
            pass
        answer[turn] = lookup(query).reshape(CORES, SPOTS, SLOTS, WIDTH)
        for there, twin in [(t, c) for t in (0, 1, 4, 2, 5, 8, 3, 6, 9, 12, 7, 10, 13, 11, 14, 15) for c in range(CORES)]:
                other = turns[turn] * CORES + twin

                def reply(there=there, twin=twin, other=other, turn=turn):
                    pltpu.make_async_remote_copy(
                        src_ref=answer.at[turn, twin, there],
                        dst_ref=got.at[me],
                        send_sem=ans_send,
                        recv_sem=ans_recv,
                        device_id=device(other, there),
                        device_id_type=MESH,
                    ).start()

                if True:
                    pl.when(jnp.logical_or(other != line, there != spot))(reply)
                else:
                    reply()

    got[me] = answer[plane, core, spot]

    landed = got.at[pl.ds(0, DEVICES - 1)]
    pltpu.make_async_copy(landed, landed, ans_recv).wait()
    out_ref[...] = jnp.dot(
        place[...],
        got[...].reshape(DEVICES * SLOTS, WIDTH),
        preferred_element_type=jnp.float32,
    ).astype(jnp.bfloat16)

    sent = ask.at[pl.ds(0, DEVICES - 1)]
    pltpu.make_async_copy(sent, sent, key_send).wait()
    pltpu.make_async_copy(landed, landed, ans_send).wait()


def on_device(fact_keys, dim_keys, dim_payload):
    whole = pl.BlockSpec(memory_space=pl.ANY)
    return pl.pallas_call(
        kernel,
        out_shape=pltpu.VMEM((FACTS, WIDTH), jnp.bfloat16),
        in_specs=[whole, whole, whole],
        out_specs=pl.BlockSpec(memory_space=pltpu.VMEM),
        scratch_shapes=[
            pltpu.VMEM((2, 128), jnp.int32),
            pltpu.VMEM((BLOCK // 128, 128), jnp.int32),
            pltpu.VMEM((BLOCK, WIDTH), jnp.bfloat16),
            pltpu.VMEM((16, BLOCK), jnp.bfloat16),
            pltpu.VMEM((DEVICES, 1, 128), jnp.float32),
            pltpu.VMEM((LINES, SPOTS, 1, 128), jnp.float32),
            pltpu.VMEM((PLANES, CORES, SPOTS, SLOTS, WIDTH), jnp.bfloat16),
            pltpu.VMEM((DEVICES, SLOTS, WIDTH), jnp.bfloat16),
            pltpu.VMEM((FACTS, DEVICES * SLOTS), jnp.bfloat16),
            pltpu.SemaphoreType.DMA((3,)),
            pltpu.SemaphoreType.DMA,
            pltpu.SemaphoreType.DMA((PLANES,)),
            pltpu.SemaphoreType.DMA,
            pltpu.SemaphoreType.DMA,
        ],
        compiler_params=pltpu.CompilerParams(collective_id=0, has_side_effects=True),
    )(fact_keys.reshape(2, 128), dim_keys.reshape(BLOCK // 128, 128), dim_payload)


def solution(mesh):
    return jax.shard_map(
        on_device,
        mesh=mesh,
        in_specs=(P(("row", "col")), P(("row", "col")), P(("row", "col"), None)),
        out_specs=P(("row", "col"), None),
        check_vma=False,
    )
```

time: 26.3 us -> 24.9 us (0.947)
  the two profiles are of different devices: /device:TPU:7 before, /device:TPU:1 now
where the time goes in v4:
time: 24.9 us; the launch traced here: 24.8 us
  Pallas kernels  24.1 us (97%)
  local copies, waits for them, and re-layouts  0.66 us (3%)
    pallas_call x1, Pallas kernels, on_device(): pl.pallas_call(kernel, out_shape=pltpu.VMEM((FACTS, WIDTH), jnp.bfloat16)...  24.1 us
    unnamed x1, local copies, waits for them, and re-layouts  0.66 us

profile of v4, /device:TPU:1, one launch (start us, length us, event | category | flops | bytes accessed | tf_op | source)
XLA Modules:
  0.0 24.8 jit_solution(13516696112913893804)
XLA Ops:
  0.0 24.1 %shard_map.37 = bf16[256,256]{1,0:T(8,128)(2,1)S(1)} custom-call(s32[2,128]{1,0:T(2,128)} %bitcast.3, s32[32,128]{1,0:T(8,128)} %bitcast.2, bf16[4096,256]{1,0:T(8,128)(2,1)} %payload_ref.1), custom_call_target="tpu_custom_call" | custom-call | tf_op jit(solution)/shard_map/pallas_call | solution.py:233
  24.1 0.7 %copy.5 = bf16[256,256]{1,0:T(8,128)(2,1)} copy(bf16[256,256]{1,0:T(8,128)(2,1)S(1)} %shard_map.37) | data formatting | bytes 262144

commit v5 on v4

--- a/solution.py
+++ b/solution.py
@@ -20,6 +20,12 @@
 WIDTH = 256
 STEP = 512
 COUNT = CORES * SPOTS
+EARLY = (0,)
+FARS = (1, 2, 3, 0)
+FIRST = tuple(
+    (0,) + tuple((z + far) % PLANES for far in FARS if (z + far) % PLANES) for z in range(PLANES)
+)
+INNER = ((0, 1), (0, 0), (1, 1), (1, 0), (4, 1), (4, 0), (2, 1), (2, 0), (5, 1), (5, 0), (8, 1), (8, 0), (3, 1), (3, 0), (6, 1), (6, 0), (9, 1), (9, 0), (12, 1), (12, 0), (7, 1), (7, 0), (10, 1), (10, 0), (13, 1), (13, 0), (11, 1), (11, 0), (14, 1), (14, 0), (15, 1), (15, 0))
 
 
 def code_of(offset):
@@ -63,6 +69,9 @@
     z, y = col // SIDE, lax.rem(col, SIDE)
     line, spot = z * CORES + core, x * SIDE + y
     plane = z
+    early = jnp.int32(0)
+    for there in EARLY:
+        early = jnp.where(spot == there, 1, early)
 
     def device(line, spot):
         return (
@@ -115,7 +124,7 @@
                     src_ref=ask.at[other * SPOTS + there],
                     dst_ref=asked.at[line, spot],
                     send_sem=key_send,
-                    recv_sem=key_recv.at[plane],
+                    recv_sem=key_recv.at[plane + PLANES * early],
                     device_id=device(other, there),
                     device_id_type=MESH,
                 ).start()
@@ -142,19 +151,43 @@
     picked = iota((COUNT, SLOTS, 128), 2) == iota((COUNT, SLOTS, 128), 1)
     ones = jnp.ones((128, 128), jnp.bfloat16)
     rows = COUNT * SLOTS
-    turns = [0, 1, 2, 3]
+    layers = [lax.rem(plane + far, PLANES) for far in FARS]
+
+    firsts = []
+    for turn in range(PLANES):
+        first = jnp.int32(FIRST[0][turn])
+        for other in range(1, PLANES):
+            first = jnp.where(plane == other, FIRST[other][turn], first)
+        firsts.append(first)
+
+    def layer_of(turn, there):
+        return firsts[turn] if there in EARLY else layers[turn]
 
     def wait_for(turn):
-        def arrive(count):
+        def arrive(layer, group, count):
             block = ask.at[pl.ds(0, count)]
-            pltpu.make_async_copy(block, block, key_recv.at[turns[turn]]).wait()
-
-
-        pl.when(plane == turns[turn])(lambda: arrive(COUNT - 1))
-        pl.when(plane != turns[turn])(lambda: arrive(COUNT))
+            pltpu.make_async_copy(block, block, key_recv.at[layer + PLANES * group]).wait()
+
+        many = CORES * len(EARLY)
+        here = jnp.logical_and(plane == firsts[turn], early == 1)
+        if many:
+            pl.when(here)(lambda: arrive(firsts[turn], 1, many - 1))
+            pl.when(jnp.logical_not(here))(lambda: arrive(firsts[turn], 1, many))
+        if FARS[turn]:
+            arrive(layers[turn], 0, COUNT - many)
+        else:
+            pl.when(early == 0)(lambda: arrive(layers[turn], 0, COUNT - many - 1))
+            pl.when(early == 1)(lambda: arrive(layers[turn], 0, COUNT - many))
 
     def queries(turn):
-        block = asked[pl.ds(turns[turn] * CORES, CORES)].reshape(COUNT, 1, 128)
+        block = jnp.concatenate(
+            [
+                asked[layer_of(turn, there) * CORES + twin, there : there + 1]
+                for twin in range(CORES)
+                for there in range(SPOTS)
+            ],
+            axis=0,
+        )
         spread = jnp.where(picked, jnp.broadcast_to(block, (COUNT, SLOTS, 128)), 0.0)
         return jnp.dot(
             spread.reshape(rows, 128).astype(jnp.bfloat16),
@@ -195,8 +228,8 @@
         else:
             pass
         answer[turn] = lookup(query).reshape(CORES, SPOTS, SLOTS, WIDTH)
-        for there, twin in [(t, c) for t in (0, 1, 4, 2, 5, 8, 3, 6, 9, 12, 7, 10, 13, 11, 14, 15) for c in range(CORES)]:
-                other = turns[turn] * CORES + twin
+        for there, twin in INNER:
+                other = layer_of(turn, there) * CORES + twin
 
                 def reply(there=there, twin=twin, other=other, turn=turn):
                     pltpu.make_async_remote_copy(
@@ -208,12 +241,16 @@
                         device_id_type=MESH,
                     ).start()
 
-                if True:
+                if there in EARLY or not FARS[turn]:
                     pl.when(jnp.logical_or(other != line, there != spot))(reply)
                 else:
                     reply()
 
-    got[me] = answer[plane, core, spot]
+    own = jnp.int32(FARS.index(0))
+    for turn in range(PLANES):
+        here = jnp.logical_and(early == 1, plane == firsts[turn])
+        own = jnp.where(here, turn, own)
+    got[me] = answer[own, core, spot]
 
     landed = got.at[pl.ds(0, DEVICES - 1)]
     pltpu.make_async_copy(landed, landed, ans_recv).wait()
@@ -247,7 +284,7 @@
             pltpu.VMEM((FACTS, DEVICES * SLOTS), jnp.bfloat16),
             pltpu.SemaphoreType.DMA((3,)),
             pltpu.SemaphoreType.DMA,
-            pltpu.SemaphoreType.DMA((PLANES,)),
+            pltpu.SemaphoreType.DMA((2 * PLANES,)),
             pltpu.SemaphoreType.DMA,
             pltpu.SemaphoreType.DMA,
         ],

time: 24.9 us -> 24.5 us (0.984)
  Pallas kernels: 24.1 us -> 23.8 us
    pallas_call x1, Pallas kernels: 24.1 us -> 23.8 us  [on_device(): pl.pallas_call(kernel, out_shape=pltpu.VMEM((FACTS, WIDTH), jnp.bfloat16)...]
where the time goes in v5:
time: 24.5 us; the launch traced here: 24.4 us
  Pallas kernels  23.8 us (97%)
  local copies, waits for them, and re-layouts  0.66 us (3%)
    pallas_call x1, Pallas kernels, on_device(): pl.pallas_call(kernel, out_shape=pltpu.VMEM((FACTS, WIDTH), jnp.bfloat16)...  23.8 us
    unnamed x1, local copies, waits for them, and re-layouts  0.66 us

profile of v5, /device:TPU:1, one launch (start us, length us, event | category | flops | bytes accessed | tf_op | source)
XLA Modules:
  0.0 24.4 jit_solution(14960905580293334136)
XLA Ops:
  0.0 23.8 %shard_map.37 = bf16[256,256]{1,0:T(8,128)(2,1)S(1)} custom-call(s32[2,128]{1,0:T(2,128)} %bitcast.3, s32[32,128]{1,0:T(8,128)} %bitcast.2, bf16[4096,256]{1,0:T(8,128)(2,1)} %payload_ref.1), custom_call_target="tpu_custom_call" | custom-call | tf_op jit(solution)/shard_map/pallas_call | solution.py:270
  23.8 0.7 %copy.5 = bf16[256,256]{1,0:T(8,128)(2,1)} copy(bf16[256,256]{1,0:T(8,128)(2,1)S(1)} %shard_map.37) | data formatting | bytes 262144

commit v6 on v5

--- a/solution.py
+++ b/solution.py
@@ -22,6 +22,9 @@
 COUNT = CORES * SPOTS
 EARLY = (0,)
 FARS = (1, 2, 3, 0)
+LAST = (3, 1, 0, 2)
+ASK_LINES = (5, 4, 7, 6, 3, 2, 1, 0)
+ASK_SPOTS = (10, 6, 9, 11, 14, 2, 5, 7, 8, 13, 15, 1, 3, 4, 12, 0)
 FIRST = tuple(
     (0,) + tuple((z + far) % PLANES for far in FARS if (z + far) % PLANES) for z in range(PLANES)
 )
@@ -64,10 +67,10 @@
 ):
     row = lax.axis_index("row")
     col = lax.axis_index("col")
-    me = row * COLS + col
     x, core = row // CORES, lax.rem(row, CORES)
     z, y = col // SIDE, lax.rem(col, SIDE)
     line, spot = z * CORES + core, x * SIDE + y
+    mine = line * SPOTS + spot
     plane = z
     early = jnp.int32(0)
     for there in EARLY:
@@ -116,8 +119,8 @@
 
     pl.semaphore_wait(barrier, DEVICES - 1)
 
-    for other in range(LINES):
-        for there in range(SPOTS):
+    for other in ASK_LINES:
+        for there in ASK_SPOTS:
 
             def request(other=other, there=there):
                 pltpu.make_async_remote_copy(
@@ -131,7 +134,7 @@
 
             pl.when(jnp.logical_or(other != line, there != spot))(request)
 
-    slot_row = owner * SLOTS + rank
+    slot_row = target * SLOTS + rank
     same = iota((FACTS, FACTS), 0) == iota((FACTS, FACTS), 1)
     slot = jnp.sum(
         jnp.where(same, slot_row.astype(jnp.float32), 0.0), axis=1, keepdims=True
@@ -234,9 +237,9 @@
                 def reply(there=there, twin=twin, other=other, turn=turn):
                     pltpu.make_async_remote_copy(
                         src_ref=answer.at[turn, twin, there],
-                        dst_ref=got.at[me],
+                        dst_ref=got.at[mine],
                         send_sem=ans_send,
-                        recv_sem=ans_recv,
+                        recv_sem=ans_recv.at[plane],
                         device_id=device(other, there),
                         device_id_type=MESH,
                     ).start()
@@ -250,15 +253,24 @@
     for turn in range(PLANES):
         here = jnp.logical_and(early == 1, plane == firsts[turn])
         own = jnp.where(here, turn, own)
-    got[me] = answer[own, core, spot]
+    got[mine] = answer[own, core, spot]
 
     landed = got.at[pl.ds(0, DEVICES - 1)]
-    pltpu.make_async_copy(landed, landed, ans_recv).wait()
-    out_ref[...] = jnp.dot(
-        place[...],
-        got[...].reshape(DEVICES * SLOTS, WIDTH),
-        preferred_element_type=jnp.float32,
-    ).astype(jnp.bfloat16)
+    total = [jnp.zeros((FACTS // 2, WIDTH), jnp.float32)] * 2
+    for far in LAST:
+        layer = lax.rem(plane + far, PLANES)
+        block = got.at[pl.ds(0, COUNT if far else COUNT - 1)]
+        pltpu.make_async_copy(block, block, ans_recv.at[layer]).wait()
+        fetched = got[pl.ds(layer * COUNT, COUNT)].reshape(rows, WIDTH)
+        spots = pl.ds(pl.multiple_of(layer * rows, rows), rows)
+        for half in range(2):
+            part = slice(half * (FACTS // 2), (half + 1) * (FACTS // 2))
+            total[half] = total[half] + jnp.dot(
+                place[part, spots], fetched, preferred_element_type=jnp.float32
+            )
+    for half in range(2):
+        part = slice(half * (FACTS // 2), (half + 1) * (FACTS // 2))
+        out_ref[part, :] = total[half].astype(jnp.bfloat16)
 
     sent = ask.at[pl.ds(0, DEVICES - 1)]
     pltpu.make_async_copy(sent, sent, key_send).wait()
@@ -286,7 +298,7 @@
             pltpu.SemaphoreType.DMA,
             pltpu.SemaphoreType.DMA((2 * PLANES,)),
             pltpu.SemaphoreType.DMA,
-            pltpu.SemaphoreType.DMA,
+            pltpu.SemaphoreType.DMA((PLANES,)),
         ],
         compiler_params=pltpu.CompilerParams(collective_id=0, has_side_effects=True),
     )(fact_keys.reshape(2, 128), dim_keys.reshape(BLOCK // 128, 128), dim_payload)

time: 24.5 us -> 24.4 us (level)
  no operation moved by 1% of the time
where the time goes in v6:
time: 24.4 us; the launch traced here: 24.2 us
  Pallas kernels  23.6 us (97%)
  local copies, waits for them, and re-layouts  0.66 us (3%)
    pallas_call x1, Pallas kernels, on_device(): pl.pallas_call(kernel, out_shape=pltpu.VMEM((FACTS, WIDTH), jnp.bfloat16)...  23.6 us
    unnamed x1, local copies, waits for them, and re-layouts  0.66 us

profile of v6, /device:TPU:1, one launch (start us, length us, event | category | flops | bytes accessed | tf_op | source)
XLA Modules:
  0.0 24.2 jit_solution(14593826367221184532)
XLA Ops:
  0.0 23.6 %shard_map.37 = bf16[256,256]{1,0:T(8,128)(2,1)S(1)} custom-call(s32[2,128]{1,0:T(2,128)} %bitcast.3, s32[32,128]{1,0:T(8,128)} %bitcast.2, bf16[4096,256]{1,0:T(8,128)(2,1)} %payload_ref.1), custom_call_target="tpu_custom_call" | custom-call | tf_op jit(solution)/shard_map/pallas_call | solution.py:282
  23.6 0.7 %copy.5 = bf16[256,256]{1,0:T(8,128)(2,1)} copy(bf16[256,256]{1,0:T(8,128)(2,1)S(1)} %shard_map.37) | data formatting | bytes 262144

commit v7 on v6

--- a/solution.py
+++ b/solution.py
@@ -23,7 +23,7 @@
 EARLY = (0,)
 FARS = (1, 2, 3, 0)
 LAST = (3, 1, 0, 2)
-ASK_LINES = (5, 4, 7, 6, 3, 2, 1, 0)
+ASK_LINES = (4, 5, 6, 7, 2, 3, 0, 1)
 ASK_SPOTS = (10, 6, 9, 11, 14, 2, 5, 7, 8, 13, 15, 1, 3, 4, 12, 0)
 FIRST = tuple(
     (0,) + tuple((z + far) % PLANES for far in FARS if (z + far) % PLANES) for z in range(PLANES)

time: 24.4 us -> 24.3 us (level)
  no operation moved by 1% of the time
where the time goes in v7:
time: 24.3 us; the launch traced here: 24.2 us
  Pallas kernels  23.6 us (97%)
  local copies, waits for them, and re-layouts  0.66 us (3%)
    pallas_call x1, Pallas kernels, on_device(): pl.pallas_call(kernel, out_shape=pltpu.VMEM((FACTS, WIDTH), jnp.bfloat16)...  23.6 us
    unnamed x1, local copies, waits for them, and re-layouts  0.66 us

profile of v7, /device:TPU:1, one launch (start us, length us, event | category | flops | bytes accessed | tf_op | source)
XLA Modules:
  0.0 24.2 jit_solution(9811828813567166285)
XLA Ops:
  0.0 23.6 %shard_map.37 = bf16[256,256]{1,0:T(8,128)(2,1)S(1)} custom-call(s32[2,128]{1,0:T(2,128)} %bitcast.3, s32[32,128]{1,0:T(8,128)} %bitcast.2, bf16[4096,256]{1,0:T(8,128)(2,1)} %payload_ref.1), custom_call_target="tpu_custom_call" | custom-call | tf_op jit(solution)/shard_map/pallas_call | solution.py:282
  23.6 0.7 %copy.5 = bf16[256,256]{1,0:T(8,128)(2,1)} copy(bf16[256,256]{1,0:T(8,128)(2,1)S(1)} %shard_map.37) | data formatting | bytes 262144

commit v8 on v6

--- a/solution.py
+++ b/solution.py
@@ -85,7 +85,7 @@
     load_facts = pltpu.make_async_copy(fact_hbm, facts, copy_sem.at[0])
     load_facts.start()
     barrier = pltpu.get_barrier_semaphore()
-    for other in range(LINES):
+    for other in (1, 0, 3, 2, 5, 4, 7, 6):
         for there in range(SPOTS):
 
             def greet(other=other, there=there):

time: 24.4 us -> 24.5 us (level)
  no operation moved by 1% of the time
where the time goes in v8:
time: 24.5 us; the launch traced here: 24.3 us
  Pallas kernels  23.6 us (96%)
  local copies, waits for them, and re-layouts  0.66 us (3%)
    pallas_call x1, Pallas kernels, on_device(): pl.pallas_call(kernel, out_shape=pltpu.VMEM((FACTS, WIDTH), jnp.bfloat16)...  23.6 us
    unnamed x1, local copies, waits for them, and re-layouts  0.66 us

profile of v8, /device:TPU:1, one launch (start us, length us, event | category | flops | bytes accessed | tf_op | source)
XLA Modules:
  0.0 24.3 jit_solution(15362958881110506117)
XLA Ops:
  0.0 23.6 %shard_map.37 = bf16[256,256]{1,0:T(8,128)(2,1)S(1)} custom-call(s32[2,128]{1,0:T(2,128)} %bitcast.3, s32[32,128]{1,0:T(8,128)} %bitcast.2, bf16[4096,256]{1,0:T(8,128)(2,1)} %payload_ref.1), custom_call_target="tpu_custom_call" | custom-call | tf_op jit(solution)/shard_map/pallas_call | solution.py:282
  23.6 0.7 %copy.5 = bf16[256,256]{1,0:T(8,128)(2,1)} copy(bf16[256,256]{1,0:T(8,128)(2,1)S(1)} %shard_map.37) | data formatting | bytes 262144

commit v9 on v6

--- a/solution.py
+++ b/solution.py
@@ -22,7 +22,7 @@
 COUNT = CORES * SPOTS
 EARLY = (0,)
 FARS = (1, 2, 3, 0)
-LAST = (3, 1, 0, 2)
+LAST = (3, 0, 1, 2)
 ASK_LINES = (5, 4, 7, 6, 3, 2, 1, 0)
 ASK_SPOTS = (10, 6, 9, 11, 14, 2, 5, 7, 8, 13, 15, 1, 3, 4, 12, 0)
 FIRST = tuple(

time: 24.4 us -> 24.5 us (level)
  no operation moved by 1% of the time
where the time goes in v9:
time: 24.5 us; the launch traced here: 24.2 us
  Pallas kernels  23.6 us (96%)
  local copies, waits for them, and re-layouts  0.66 us (3%)
    pallas_call x1, Pallas kernels, on_device(): pl.pallas_call(kernel, out_shape=pltpu.VMEM((FACTS, WIDTH), jnp.bfloat16)...  23.6 us
    unnamed x1, local copies, waits for them, and re-layouts  0.66 us

profile of v9, /device:TPU:1, one launch (start us, length us, event | category | flops | bytes accessed | tf_op | source)
XLA Modules:
  0.0 24.2 jit_solution(4880752384035375246)
XLA Ops:
  0.0 23.6 %shard_map.37 = bf16[256,256]{1,0:T(8,128)(2,1)S(1)} custom-call(s32[2,128]{1,0:T(2,128)} %bitcast.3, s32[32,128]{1,0:T(8,128)} %bitcast.2, bf16[4096,256]{1,0:T(8,128)(2,1)} %payload_ref.1), custom_call_target="tpu_custom_call" | custom-call | tf_op jit(solution)/shard_map/pallas_call | solution.py:282
  23.6 0.7 %copy.5 = bf16[256,256]{1,0:T(8,128)(2,1)} copy(bf16[256,256]{1,0:T(8,128)(2,1)S(1)} %shard_map.37) | data formatting | bytes 262144
